TPU v7x, 32 devices: a whole 2x2x4 slice. The times are simulated.
32 devices in a mesh: robot: 8 (over z, x), sub: 4 (over y, core).
Axes of the slice: x: 2, y: 2, z: 4, core: 2. Of those that a mesh axis runs over, the one named last changes fastest.
Arguments:
- landmark_copies: float32 [8, 4, 3, 512], P('robot', 'sub'), may hold values from -6 to 6
- dual_copies: float32 [8, 4, 3, 512], P('robot', 'sub'), may hold values from -4 to 4
- visibility: int32 [8, 4, 512], P('robot', 'sub'), may hold values from 0 to 511
- block_counts: int32 [8, 4, 8], P('robot', 'sub'), may hold values from 1 to 64, as said below
- consensus_old: float32 [8, 4, 3, 512], P('robot', 'sub'), may hold values from -6 to 6
- poses: float32 [8, 4, 6, 1024], P('robot', 'sub'), may hold values from -6 to 6
- inverse_blocks: float32 [8, 4, 36, 1024], P('robot', 'sub'), may hold values from -1.8 to 1.8
- jacobians: float32 [8, 4, 18, 4096], P('robot', 'sub'), may hold values from -3 to 3
- measurements: float32 [8, 4, 3, 4096], P('robot', 'sub'), may hold values from -6 to 6
- obs_pose: int32 [8, 4, 4096], P('robot', 'sub'), may hold values from 0 to 1023
- obs_slot: int32 [8, 4, 4096], P('robot', 'sub'), may hold values from 0 to 511, as said below
- edge_to: int32 [8, 4, 1024], P('robot', 'sub'), may hold values from 0 to 4095
- edge_offset: float32 [8, 4, 6, 1024], P('robot', 'sub'), may hold values from -3 to 3
Outputs:
- refined_poses: float32 [8, 4, 6, 1024], P('robot', 'sub')
- consensus: float32 [8, 4, 3, 512], P('robot', 'sub')
- dual_new: float32 [8, 4, 3, 512], P('robot', 'sub')
- residual_norms: float32 [2], replicated
Inputs may be any that keep to these rules, and one draw needn't show every extreme that they name: block_counts[r,s,d] counts the live slots at the head of block d; for every sub index some robot receives full blocks from every robot, which robot varies with the draw. `obs_slot`: each observation names a live slot of its own device.
All inputs are finite; a program needn't handle non-finite values.
Results may differ from a plain program's by a relative error of at most 0.0001.
Values sent between devices are 32-bit elements; how exact they have to be, the bound alone decides.
No kernel may reach another device: no remote copies, remote signals or barrier semaphores. Data moves between devices by JAX's collectives and lax.ppermute only.
A program may use at most 64 MiB of HBM per device.

v0:
```python
import jax
import jax.numpy as jnp
from jax import lax
from jax.sharding import PartitionSpec as P

penalty = 2.0


def body(
    landmark_copies,
    dual_copies,
    visibility,
    block_counts,
    consensus_old,
    poses,
    inverse_blocks,
    jacobians,
    measurements,
    obs_pose,
    obs_slot,
    edge_to,
    edge_offset,
):
    copies = landmark_copies[0, 0]
    duals = dual_copies[0, 0]
    slot_ids = visibility[0]
    counts = block_counts[0, 0]
    old_estimate = consensus_old[0, 0]
    robots = lax.axis_size("robot")
    slot_count = copies.shape[1]
    block_size = slot_count // robots
    owned = old_estimate.shape[1]
    live_mask = (
        (jnp.arange(block_size)[None, :] < counts[:, None]).reshape(slot_count).astype(jnp.float32)
    )
    outgoing = jnp.concatenate([(copies + duals) * live_mask[None, :], live_mask[None, :]], axis=0)
    received, received_ids = (
        lax.all_to_all(outgoing, "robot", split_axis=1, concat_axis=1, tiled=True),
        lax.all_to_all(slot_ids, "robot", split_axis=1, concat_axis=1, tiled=True),
    )
    owner_ids = received_ids[0]
    totals = jax.vmap(lambda entries: jax.ops.segment_sum(entries, owner_ids, num_segments=owned))(
        received
    )
    consensus = (old_estimate + totals[:3]) / (1.0 + totals[3:4])
    returning = consensus[:, owner_ids]
    back = lax.all_to_all(returning, "robot", split_axis=1, concat_axis=1, tiled=True)
    differ = (copies - back) * live_mask[None, :]
    dual_new = duals + differ
    primal = jnp.sum(differ * differ)
    change = consensus - old_estimate
    dualsum = penalty * penalty * jnp.sum(totals[3:4] * change * change)
    primal_all, dual_all = lax.psum((primal, dualsum), ("robot", "sub"))
    landmark_total = owned * robots * lax.axis_size("sub")
    residual_norms = jnp.sqrt(jnp.stack([primal_all, dual_all]) / landmark_total)
    pose_block = poses[0, 0]
    pose_count = pose_block.shape[1]
    robot_all = lax.all_gather(pose_block, "sub", axis=1, tiled=True)
    pose_far = robot_all[:, edge_to[0, 0]]
    copies_at = copies[:, obs_slot[0, 0]]
    error = measurements[0, 0] - copies_at
    jac_rows = jacobians[0, 0].reshape(3, 6, error.shape[1])
    pull = jnp.sum(jac_rows * error[:, None, :], axis=0)
    pose_ids = obs_pose[0, 0]
    grad_obs = jax.vmap(
        lambda entries: jax.ops.segment_sum(entries, pose_ids, num_segments=pose_count)
    )(pull)
    grad = grad_obs + pose_far - pose_block - edge_offset[0, 0]
    inverse = inverse_blocks[0, 0].reshape(6, 6, pose_count)
    delta = jnp.sum(inverse * grad[None, :, :], axis=1)
    refined = pose_block + delta
    return (refined[None, None], consensus[None, None], dual_new[None, None], residual_norms)


def solution(mesh):
    return jax.shard_map(
        body,
        mesh=mesh,
        in_specs=(
            P("robot", "sub", None, None),
            P("robot", "sub", None, None),
            P("robot", "sub", None),
            P("robot", "sub", None),
            P("robot", "sub", None, None),
            P("robot", "sub", None, None),
            P("robot", "sub", None, None),
            P("robot", "sub", None, None),
            P("robot", "sub", None, None),
            P("robot", "sub", None),
            P("robot", "sub", None),
            P("robot", "sub", None),
            P("robot", "sub", None, None),
        ),
        out_specs=(
            P("robot", "sub", None, None),
            P("robot", "sub", None, None),
            P("robot", "sub", None, None),
            P(),
        ),
        check_vma=False,
    )
```

profile of v0, /device:TPU:0, one launch (start us, length us, event | category | flops | bytes accessed | tf_op | source)
XLA Modules:
  0.0 154.9 jit_solution(5562532823633209940)
XLA Ops:
  1.1 1.3 reduce.16
  2.5 0.7 all_to_all.22
  3.2 7.3 %all-to-all-start = ((s32[1,8,64]{2,0,1:T(1,128)}), s32[1,8,64]{2,0,1:T(1,128)S(1)}, u32[]{:S(2)}, u32[]{:S(2)}) async-start(s32[1,8,64]{2,0,1:T(1,128)} %all_to_all.22), calls=%async_computation | async-start | bytes 8192 | tf_op jit(solution)/shard_map/all_to_all | solution.py:39
  10.4 0.7 fusion.8
  11.2 0.7 fusion.9
  11.9 0.8 copy.53
  12.7 0.7 add_reduce_fusion.1
  13.6 0.7 compare_select_fusion
  14.3 1.4 copy.52
  15.7 14.1 %gather_fusion.1 = f32[4096,3]{1,0:T(8,128)} fusion(f32[3,512]{0,1:T(8,128)S(1)} %bitcast.54, s32[4096]{0:T(1024)S(1)} %broadcast_clamp_fusion), kind=kCustom, calls=%fused_computation.1 | custom fusion | bytes 114688 | tf_op jit(solution)/shard_map/gather | solution.py:60
  29.8 3.2 %bitcast_subtract_fusion = f32[3,4096]{0,1:T(8,128)} fusion(f32[4096,3]{1,0:T(8,128)} %gather_fusion.1, f32[1,1,3,4096]{2,3,1,0:T(8,128)S(1)} %copy.52), kind=kLoop, calls=%fused_computation.5 | loop fusion | flops 12288 | bytes 147456 | tf_op jit(solution)/shard_map/sub | solution.py:61
  33.0 2.3 %copy.54 = f32[3,4096]{1,0:T(4,128)S(1)} copy(f32[3,4096]{0,1:T(8,128)} %bitcast_subtract_fusion) | data formatting | bytes 98304 | tf_op jit(solution)/shard_map/sub | solution.py:61
  35.2 0.7 reduce.1
  36.1 2.0 %copy.55 = f32[4096,6]{1,0:T(8,128)} copy(f32[4096,6]{0,1:T(8,128)S(1)} %bitcast.57) | data formatting | bytes 196608 | tf_op jit(solution)/shard_map/reduce_sum | solution.py:63
  38.3 15.8 %all-gather = f32[1,1,6,4096]{2,3,1,0:T(8,128)S(1)} all-gather(f32[1,1,6,1024]{2,3,1,0:T(8,128)S(1)} %copy.51), channel_id=2, replica_groups=mesh['robot'=8,'sub'=4] {'sub'}, dimensions={3}, use_global_device_ids=true | all-gather | bytes 122880 | tf_op jit(solution)/shard_map/all_gather | solution.py:58
  54.1 1.0 copy.57
  55.1 2.8 %gather_fusion = f32[1024,6]{1,0:T(8,128)S(1)} fusion(f32[6,4096]{0,1:T(8,128)S(1)} %bitcast.55, s32[1024]{0:T(1024)S(1)} %broadcast_clamp_fusion.1), kind=kCustom, calls=%fused_computation | custom fusion | bytes 53248 | tf_op jit(solution)/shard_map/gather | solution.py:59
  58.0 22.9 %scatter_fusion = f32[6,1024]{0,1:T(8,128)S(1)} fusion(f32[6,1024]{0,1:T(8,128)S(1)} %bitcast.53, s32[4096]{0:T(1024)S(1)} %bitcast.67, f32[4096,6]{1,0:T(8,128)} %copy.55), kind=kCustom, calls=%fused_computation.3 | custom fusion | flops 24576 | bytes 311296 | tf_op jit(solution)/shard_map/vmap()/scatter-add | solution.py:66
  81.7 0.7 reshape.262
  82.6 6.0 %all-to-all-start.1 = ((f32[8,1,256]{2,1,0:T(1,128)}), f32[8,1,256]{2,1,0:T(1,128)S(1)}, u32[]{:S(2)}, u32[]{:S(2)}) async-start(f32[8,1,256]{2,1,0:T(1,128)} %reshape.262), calls=%async_computation.1 | async-start | bytes 16384 | tf_op jit(solution)/shard_map/all_to_all | solution.py:38
  89.4 5.7 %all-to-all-done.1 = f32[8,1,256]{2,1,0:T(1,128)S(1)} async-done(((f32[8,1,256]{2,1,0:T(1,128)}), f32[8,1,256]{2,1,0:T(1,128)S(1)}, u32[]{:S(2)}, u32[]{:S(2)}) %all-to-all-start.1) | async-done | bytes 8224 | tf_op jit(solution)/shard_map/all_to_all | solution.py:38
  96.6 2.3 %scatter_custom_fusion.1 = f32[4,512]{0,1:T(8,128)S(1)} fusion(s32[512]{0:T(512)S(1)} %reshape.227, f32[512,4]{1,0:T(8,128)S(1)} %copy.62, f32[]{:T(128)} %constant.10.clone.1), kind=kCustom, calls=%fused_computation.21 | custom fusion | flops 2048 | bytes 8196 | tf_op jit(solution)/shard_map/vmap()/scatter-add | solution.py:42
  99.2 0.8 fusion
  100.0 1.0 gather_fusion.2
  101.2 0.7 reshape.264
  101.9 3.3 %all-to-all-start.2 = ((f32[8,1,192]{2,1,0:T(1,128)}), f32[8,1,192]{2,1,0:T(1,128)S(1)}, u32[]{:S(2)}, u32[]{:S(2)}) async-start(f32[8,1,192]{2,1,0:T(1,128)} %reshape.264), calls=%async_computation.2 | async-start | bytes 16384 | tf_op jit(solution)/shard_map/all_to_all | solution.py:47
  106.0 0.7 copy.68
  107.3 4.4 %all-to-all-done.2 = f32[8,1,192]{2,1,0:T(1,128)S(1)} async-done(((f32[8,1,192]{2,1,0:T(1,128)}), f32[8,1,192]{2,1,0:T(1,128)S(1)}, u32[]{:S(2)}, u32[]{:S(2)}) %all-to-all-start.2) | async-done | bytes 6176 | tf_op jit(solution)/shard_map/all_to_all | solution.py:47
  111.7 0.7 reduce.19
  112.7 0.7 fusion.4
  114.1 38.9 %all-reduce = (f32[1]{0:T(128)}, f32[1]{0:T(128)}) all-reduce(f32[1]{0:T(128)} %bitcast.22, f32[1]{0:T(128)} %bitcast.21), channel_id=1, replica_groups=mesh['robot'=8,'sub'=4] {'robot','sub'}, use_global_device_ids=true, to_apply=%region_7.0 | all-reduce | flops 2 | bytes 16 | tf_op jit(solution)/shard_map/psum | solution.py:53
  153.0 1.9 %fusion.10 = f32[2]{0:T(128)} fusion(f32[1]{0:T(128)} %get-tuple-element.22, f32[1]{0:T(128)} %get-tuple-element.23), kind=kLoop, calls=%fused_computation.41 | loop fusion | flops 4 | bytes 16 | tf_op jit(solution)/shard_map/sqrt | solution.py:55
  (59 shorter events, 6.2 us)
Async XLA Ops:
  3.2 79.4 %all-to-all-start = ((s32[1,8,64]{2,0,1:T(1,128)}), s32[1,8,64]{2,0,1:T(1,128)S(1)}, u32[]{:S(2)}, u32[]{:S(2)}) async-start(s32[1,8,64]{2,0,1:T(1,128)} %all_to_all.22), calls=%async_computation | async-start | bytes 8192 | tf_op jit(solution)/shard_map/all_to_all | solution.py:39
  33.0 2.3 %copy-start.1 = (f32[1,1,18,4096]{3,1,2,0:T(1,128)S(1)}, f32[1,1,18,4096]{3,1,2,0:T(1,128)}, u32[]{:S(2)}) copy-start(f32[1,1,18,4096]{3,1,2,0:T(1,128)} %param.20) | copy-start | bytes 884740
  35.2 2.8 %copy-start.3 = (f32[1,1,6,1024]{3,1,2,0:T(1,128)S(1)}, f32[1,1,6,1024]{3,1,2,0:T(1,128)}, u32[]{:S(2)}) copy-start(f32[1,1,6,1024]{3,1,2,0:T(1,128)} %param.18) | copy-start | bytes 73732
  38.1 16.0 %copy-start.9 = (s32[1,1,1024]{2,1,0:T(1,128)S(1)}, s32[1,1,1024]{2,1,0:T(1,128)}, u32[]{:S(2)}) copy-start(s32[1,1,1024]{2,1,0:T(1,128)} %param.24) | copy-start | bytes 12292
  38.1 16.0 %copy-start.5 = (f32[1,1,6,1024]{3,1,2,0:T(1,128)S(1)}, f32[1,1,6,1024]{3,1,2,0:T(1,128)}, u32[]{:S(2)}) copy-start(f32[1,1,6,1024]{3,1,2,0:T(1,128)} %param.25) | copy-start | bytes 73732
  38.1 19.9 %copy-start.7 = (s32[1,1,4096]{2,1,0:T(1,128)S(1)}, s32[1,1,4096]{2,1,0:T(1,128)}, u32[]{:S(2)}) copy-start(s32[1,1,4096]{2,1,0:T(1,128)} %param.22) | copy-start | bytes 49156
  57.9 23.0 %copy-start = (f32[1,1,6,1024]{2,3,1,0:T(8,128)S(1)}, f32[1,1,6,1024]{2,3,1,0:T(8,128)}, u32[]{:S(2)}) copy-start(f32[1,1,6,1024]{2,3,1,0:T(8,128)} %copy.57) | copy-start | bytes 73732
  58.0 23.2 %copy-start.2 = (f32[1,1,36,1024]{3,1,2,0:T(1,128)S(1)}, f32[1,1,36,1024]{3,1,2,0:T(1,128)}, u32[]{:S(2)}) copy-start(f32[1,1,36,1024]{3,1,2,0:T(1,128)} %param.19) | copy-start | bytes 442372
  80.9 1.5 copy-start.8
  81.6 31.9 %copy-start.4 = (f32[1,1,3,512]{3,1,2,0:T(1,128)S(1)}, f32[1,1,3,512]{3,1,2,0:T(1,128)}, u32[]{:S(2)}) copy-start(f32[1,1,3,512]{3,1,2,0:T(1,128)} %param.13) | copy-start | bytes 18436
  81.6 31.9 %copy-start.6 = (f32[1,1,3,512]{3,1,2,0:T(1,128)S(1)}, f32[1,1,3,512]{3,1,2,0:T(1,128)}, u32[]{:S(2)}) copy-start(f32[1,1,3,512]{3,1,2,0:T(1,128)} %param.14) | copy-start | bytes 18436
  82.6 12.5 %all-to-all-start.1 = ((f32[8,1,256]{2,1,0:T(1,128)}), f32[8,1,256]{2,1,0:T(1,128)S(1)}, u32[]{:S(2)}, u32[]{:S(2)}) async-start(f32[8,1,256]{2,1,0:T(1,128)} %reshape.262), calls=%async_computation.1 | async-start | bytes 16384 | tf_op jit(solution)/shard_map/all_to_all | solution.py:38
  101.9 9.8 %all-to-all-start.2 = ((f32[8,1,192]{2,1,0:T(1,128)}), f32[8,1,192]{2,1,0:T(1,128)S(1)}, u32[]{:S(2)}, u32[]{:S(2)}) async-start(f32[8,1,192]{2,1,0:T(1,128)} %reshape.264), calls=%async_computation.2 | async-start | bytes 16384 | tf_op jit(solution)/shard_map/all_to_all | solution.py:47
where the time goes:
time: 156 us; the launch traced here: 155 us
  blocking collectives  54.7 us (35%)
  other arithmetic  40.4 us (26%)
  local copies, waits for them, and re-layouts  31.6 us (20%)
  starting transfers between devices  16.6 us (11%)
  waiting for transfers between devices  10.1 us (6%)
  between operations  1.6 us (1%)
    psum x1, blocking collectives, body(): primal_all, dual_all = lax.psum((primal, dualsum), ('robot', 'sub'))  38.9 us
    scatter-add x1, other arithmetic, body(): jax.ops.segment_sum(entries, pose_ids, num_segments=pose_count)  22.9 us
    all_gather x1, blocking collectives, body(): robot_all = lax.all_gather(pose_block, 'sub', axis=1, tiled=True)  15.8 us
    gather x1, local copies, waits for them, and re-layouts, body(): copies_at = copies[:, obs_slot[0, 0]]  14.1 us
    all_to_all x1, starting transfers between devices, body(): lax.all_to_all(slot_ids, 'robot', split_axis=1, concat_axis=1, tiled=True)  7.28 us
    unnamed x32, local copies, waits for them, and re-layouts  7.06 us
    all_to_all x1, starting transfers between devices, body(): lax.all_to_all(outgoing, 'robot', split_axis=1, concat_axis=1, tiled=True)  6.01 us
    all_to_all x1, waiting for transfers between devices, body(): lax.all_to_all(outgoing, 'robot', split_axis=1, concat_axis=1, tiled=True)  5.69 us
  transfers between devices with their start and end apart: 3, of which 2 were waited for; matrix products, arithmetic and copies ran while one was open for 38% of the time, Pallas kernels for 0%

commit v1 on v0

--- a/solution.py
+++ b/solution.py
@@ -55,7 +55,12 @@
     residual_norms = jnp.sqrt(jnp.stack([primal_all, dual_all]) / landmark_total)
     pose_block = poses[0, 0]
     pose_count = pose_block.shape[1]
-    robot_all = lax.all_gather(pose_block, "sub", axis=1, tiled=True)
+    ring = [pose_block]
+    for hop in range(3):
+        ring.append(lax.ppermute(ring[-1], "sub", [(dev, (dev + 1) % 4) for dev in range(4)]))
+    robot_all = jnp.roll(
+        jnp.concatenate(ring[::-1], axis=1), (lax.axis_index("sub") + 1) * ring[0].shape[1], axis=1
+    )
     pose_far = robot_all[:, edge_to[0, 0]]
     copies_at = copies[:, obs_slot[0, 0]]
     error = measurements[0, 0] - copies_at

time: 156 us -> 148 us (0.949)
  blocking collectives: 54.7 us -> 40.7 us
  waiting for transfers between devices: 10.1 us -> 12.6 us
  other arithmetic: 40.4 us -> 42.4 us
    all_gather x1 -> x0, blocking collectives: 15.8 us -> none  [body(): robot_all = lax.all_gather(pose_block, 'sub', axis=1, tiled=True)]
    ppermute x0 -> x3, waiting for transfers between devices: none -> 6.12 us  [body(): lax.ppermute(ring[-1], 'sub', [(dev, (dev + 1) % 4) for dev in range(4)])]
    all_to_all x1, waiting for transfers between devices: 4.39 us -> 0.81 us  [body(): lax.all_to_all(returning, 'robot', split_axis=1, concat_axis=1, tiled=True)]
    unnamed x32 -> x35, local copies, waits for them, and re-layouts: 7.06 us -> 9.34 us
    psum x1, blocking collectives: 38.9 us -> 40.7 us  [body(): primal_all, dual_all = lax.psum((primal, dualsum), ('robot', 'sub'))]
    sub x1, local copies, waits for them, and re-layouts: 2.25 us -> 0.62 us  [body(): error = measurements[0, 0] - copies_at]
  transfers between devices with their start and end apart: 3 -> 6, of which waited for: 2 -> 3; matrix products, arithmetic and copies ran while one was open for 38% -> 31% of each run, Pallas kernels for 0% -> 0%
where the time goes in v1:
time: 148 us; the launch traced here: 147 us
  other arithmetic  42.4 us (29%)
  blocking collectives  40.7 us (28%)
  local copies, waits for them, and re-layouts  33.1 us (22%)
  starting transfers between devices  16.8 us (11%)
  waiting for transfers between devices  12.6 us (9%)
  between operations  1.65 us (1%)
    psum x1, blocking collectives, body(): primal_all, dual_all = lax.psum((primal, dualsum), ('robot', 'sub'))  40.7 us
    scatter-add x1, other arithmetic, body(): jax.ops.segment_sum(entries, pose_ids, num_segments=pose_count)  22.9 us
    gather x1, local copies, waits for them, and re-layouts, body(): copies_at = copies[:, obs_slot[0, 0]]  14.1 us
    unnamed x35, local copies, waits for them, and re-layouts  9.34 us
    all_to_all x1, starting transfers between devices, body(): lax.all_to_all(slot_ids, 'robot', split_axis=1, concat_axis=1, tiled=True)  6.8 us
    ppermute x3, waiting for transfers between devices, body(): lax.ppermute(ring[-1], 'sub', [(dev, (dev + 1) % 4) for dev in range(4)])  6.12 us
    all_to_all x1, starting transfers between devices, body(): lax.all_to_all(outgoing, 'robot', split_axis=1, concat_axis=1, tiled=True)  6.01 us
    all_to_all x1, waiting for transfers between devices, body(): lax.all_to_all(outgoing, 'robot', split_axis=1, concat_axis=1, tiled=True)  5.69 us
  transfers between devices with their start and end apart: 6, of which 3 were waited for; matrix products, arithmetic and copies ran while one was open for 31% of the time, Pallas kernels for 0%

profile of v1, /device:TPU:0, one launch (start us, length us, event | category | flops | bytes accessed | tf_op | source)
XLA Modules:
  0.0 147.2 jit_solution(2346915817919433879)
XLA Ops:
  0.6 1.0 copy.84
  2.6 1.3 reduce.16
  4.7 6.8 %all-to-all-start = ((s32[1,8,64]{2,0,1:T(1,128)}), s32[1,8,64]{2,0,1:T(1,128)S(1)}, u32[]{:S(2)}, u32[]{:S(2)}) async-start(s32[1,8,64]{2,0,1:T(1,128)} %all_to_all.22), calls=%async_computation | async-start | bytes 8192 | tf_op jit(solution)/shard_map/all_to_all | solution.py:39
  11.5 0.7 fusion.8
  12.2 0.7 fusion.9
  12.9 0.7 compare_select_fusion.1
  13.6 0.8 copy.86
  14.5 0.7 compare_select_fusion
  15.2 2.7 %copy.85 = f32[1,1,3,4096]{2,3,1,0:T(8,128)} copy(f32[1,1,3,4096]{3,1,2,0:T(1,128)} %param.21) | data formatting | bytes 98304 | tf_op args[8]
  17.9 0.7 add_reduce_fusion.1
  18.8 14.1 %gather_fusion.1 = f32[4096,3]{1,0:T(8,128)} fusion(f32[3,512]{0,1:T(8,128)S(1)} %bitcast.54, s32[4096]{0:T(1024)S(1)} %broadcast_clamp_fusion), kind=kCustom, calls=%fused_computation.1 | custom fusion | bytes 114688 | tf_op jit(solution)/shard_map/gather | solution.py:65
  32.8 2.4 %bitcast_subtract_fusion = f32[3,4096]{0,1:T(8,128)S(1)} fusion(f32[4096,3]{1,0:T(8,128)} %gather_fusion.1, f32[1,1,3,4096]{2,3,1,0:T(8,128)} %copy.85), kind=kLoop, calls=%fused_computation.5 | loop fusion | flops 12288 | bytes 147456 | tf_op jit(solution)/shard_map/sub | solution.py:66
  36.0 1.7 %reduce.1 = f32[18,4096]{1,0:T(8,128)S(1)} reduce(f32[1,1,18,4096]{3,1,2,0:T(1,128)} %param.20, f32[]{:T(128)} %constant.61), dimensions={0,1}, to_apply=%param.20.reduce_sub_computation | reduce | bytes 589828 | tf_op args[7]
  38.6 6.0 %all-to-all-start.1 = ((f32[8,1,256]{2,1,0:T(1,128)}), f32[8,1,256]{2,1,0:T(1,128)S(1)}, u32[]{:S(2)}, u32[]{:S(2)}) async-start(f32[8,1,256]{2,1,0:T(1,128)} %reshape.261), calls=%async_computation.1 | async-start | bytes 16384 | tf_op jit(solution)/shard_map/all_to_all | solution.py:38
  45.5 5.7 %all-to-all-done.1 = f32[8,1,256]{2,1,0:T(1,128)S(1)} async-done(((f32[8,1,256]{2,1,0:T(1,128)}), f32[8,1,256]{2,1,0:T(1,128)S(1)}, u32[]{:S(2)}, u32[]{:S(2)}) %all-to-all-start.1) | async-done | bytes 8224 | tf_op jit(solution)/shard_map/all_to_all | solution.py:38
  52.7 2.3 %scatter_custom_fusion.1 = f32[4,512]{0,1:T(8,128)S(1)} fusion(s32[512]{0:T(512)S(1)} %reshape.227, f32[512,4]{1,0:T(8,128)S(1)} %copy.94, f32[]{:T(128)} %constant.44.clone.1), kind=kCustom, calls=%fused_computation.20 | custom fusion | flops 2048 | bytes 8196 | tf_op jit(solution)/shard_map/vmap()/scatter-add | solution.py:42
  55.3 0.8 fusion
  56.1 1.0 gather_fusion.2
  57.3 0.7 reshape.263
  58.0 3.3 %all-to-all-start.2 = ((f32[8,1,192]{2,1,0:T(1,128)}), f32[8,1,192]{2,1,0:T(1,128)S(1)}, u32[]{:S(2)}, u32[]{:S(2)}) async-start(f32[8,1,192]{2,1,0:T(1,128)} %reshape.263), calls=%async_computation.2 | async-start | bytes 16384 | tf_op jit(solution)/shard_map/all_to_all | solution.py:47
  61.5 2.0 %copy.88 = f32[4096,6]{1,0:T(8,128)} copy(f32[4096,6]{0,1:T(8,128)S(1)} %bitcast.56) | data formatting | bytes 196608 | tf_op jit(solution)/shard_map/reduce_sum | solution.py:68
  63.5 1.0 copy.89
  64.8 0.7 reshape_squeeze.6
  65.5 0.7 copy.100
  67.0 0.8 all-to-all-done.2
  68.8 0.7 fusion.4
  69.5 40.7 %all-reduce = (f32[1]{0:T(128)}, f32[1]{0:T(128)}) all-reduce(f32[1]{0:T(128)} %bitcast.21, f32[1]{0:T(128)} %bitcast.20), channel_id=1, replica_groups=mesh['robot'=8,'sub'=4] {'robot','sub'}, use_global_device_ids=true, to_apply=%region_7.8 | all-reduce | flops 2 | bytes 16 | tf_op jit(solution)/shard_map/psum | solution.py:53
  110.3 1.9 %fusion.10 = f32[2]{0:T(128)} fusion(f32[1]{0:T(128)} %get-tuple-element.26, f32[1]{0:T(128)} %get-tuple-element.27), kind=kLoop, calls=%fused_computation.48 | loop fusion | flops 4 | bytes 16 | tf_op jit(solution)/shard_map/sqrt | solution.py:55
  112.8 6.1 %collective-permute-done.2 = f32[6,1024]{0,1:T(8,128)S(1)} collective-permute-done((f32[6,1024]{0,1:T(8,128)S(1)}, f32[6,1024]{0,1:T(8,128)S(1)}, u32[]{:S(2)}, u32[]{:S(2)}) %collective-permute-start.2) | collective-permute-done | bytes 24608 | tf_op jit(solution)/shard_map/ppermute | solution.py:60
  119.4 2.8 %gather_fusion = f32[1024,6]{1,0:T(8,128)S(1)} fusion(f32[6,4096]{0,1:T(8,128)S(1)} %constant_dynamic-slice_fusion, s32[1024]{0:T(1024)S(1)} %get-tuple-element.31), kind=kCustom, calls=%fused_computation | custom fusion | bytes 53248 | tf_op jit(solution)/shard_map/gather | solution.py:64
  122.2 22.9 %scatter_fusion = f32[6,1024]{0,1:T(8,128)S(1)} fusion(f32[6,1024]{0,1:T(8,128)S(1)} %bitcast.53, s32[4096]{0:T(1024)S(1)} %bitcast.66, f32[4096,6]{1,0:T(8,128)} %copy.88), kind=kCustom, calls=%fused_computation.3 | custom fusion | flops 24576 | bytes 311296 | tf_op jit(solution)/shard_map/vmap()/scatter-add | solution.py:71
  145.1 1.1 bitcast_subtract_fusion.1
  (68 shorter events, 9.6 us)
Async XLA Ops:
  1.6 65.3 %collective-permute-start = (f32[6,1024]{0,1:T(8,128)S(1)}, f32[6,1024]{0,1:T(8,128)S(1)}, u32[]{:S(2)}, u32[]{:S(2)}) collective-permute-start(f32[6,1024]{0,1:T(8,128)S(1)} %bitcast.52), channel_id=1, source_target_pairs={{0,1},{1,2},{2,3},{3,0},{4,5},{5,6},{6,7},{7,4},{8,9},{9,10},{10,1... | collective-permute-start | bytes 73736 | tf_op jit(solution)/shard_map/ppermute | solution.py:60
  4.7 33.9 %all-to-all-start = ((s32[1,8,64]{2,0,1:T(1,128)}), s32[1,8,64]{2,0,1:T(1,128)S(1)}, u32[]{:S(2)}, u32[]{:S(2)}) async-start(s32[1,8,64]{2,0,1:T(1,128)} %all_to_all.22), calls=%async_computation | async-start | bytes 8192 | tf_op jit(solution)/shard_map/all_to_all | solution.py:39
  32.8 5.6 %copy-start.7 = (f32[1,1,3,512]{3,1,2,0:T(1,128)S(1)}, f32[1,1,3,512]{3,1,2,0:T(1,128)}, u32[]{:S(2)}) copy-start(f32[1,1,3,512]{3,1,2,0:T(1,128)} %param.17) | copy-start | bytes 18436
  35.3 28.1 %copy-start.4 = (f32[1,1,6,1024]{3,1,2,0:T(1,128)S(1)}, f32[1,1,6,1024]{3,1,2,0:T(1,128)}, u32[]{:S(2)}) copy-start(f32[1,1,6,1024]{3,1,2,0:T(1,128)} %param.25) | copy-start | bytes 73732
  35.9 28.5 %copy-start.1 = (f32[1,1,36,1024]{3,1,2,0:T(1,128)S(1)}, f32[1,1,36,1024]{3,1,2,0:T(1,128)}, u32[]{:S(2)}) copy-start(f32[1,1,36,1024]{3,1,2,0:T(1,128)} %param.19) | copy-start | bytes 442372
  35.9 32.8 %copy-start.3 = (f32[1,1,3,512]{3,1,2,0:T(1,128)S(1)}, f32[1,1,3,512]{3,1,2,0:T(1,128)}, u32[]{:S(2)}) copy-start(f32[1,1,3,512]{3,1,2,0:T(1,128)} %param.13) | copy-start | bytes 18436
  36.0 32.8 %copy-start.5 = (f32[1,1,3,512]{3,1,2,0:T(1,128)S(1)}, f32[1,1,3,512]{3,1,2,0:T(1,128)}, u32[]{:S(2)}) copy-start(f32[1,1,3,512]{3,1,2,0:T(1,128)} %param.14) | copy-start | bytes 18436
  38.6 12.5 %all-to-all-start.1 = ((f32[8,1,256]{2,1,0:T(1,128)}), f32[8,1,256]{2,1,0:T(1,128)S(1)}, u32[]{:S(2)}, u32[]{:S(2)}) async-start(f32[8,1,256]{2,1,0:T(1,128)} %reshape.261), calls=%async_computation.1 | async-start | bytes 16384 | tf_op jit(solution)/shard_map/all_to_all | solution.py:38
  58.0 9.8 %all-to-all-start.2 = ((f32[8,1,192]{2,1,0:T(1,128)}), f32[8,1,192]{2,1,0:T(1,128)S(1)}, u32[]{:S(2)}, u32[]{:S(2)}) async-start(f32[8,1,192]{2,1,0:T(1,128)} %reshape.263), calls=%async_computation.2 | async-start | bytes 16384 | tf_op jit(solution)/shard_map/all_to_all | solution.py:47
  66.9 43.4 %collective-permute-start.1 = (f32[6,1024]{0,1:T(8,128)S(1)}, f32[6,1024]{0,1:T(8,128)S(1)}, u32[]{:S(2)}, u32[]{:S(2)}) collective-permute-start(f32[6,1024]{0,1:T(8,128)S(1)} %collective-permute-done), channel_id=1, source_target_pairs={{0,1},{1,2},{2,3},{3,0},{4,5},{5,6},{6,7},{7,4},{8,9},{9,10},{10,1... | collective-permute-start | bytes 73736 | tf_op jit(solution)/shard_map/ppermute | solution.py:60
  110.3 8.6 %collective-permute-start.2 = (f32[6,1024]{0,1:T(8,128)S(1)}, f32[6,1024]{0,1:T(8,128)S(1)}, u32[]{:S(2)}, u32[]{:S(2)}) collective-permute-start(f32[6,1024]{0,1:T(8,128)S(1)} %collective-permute-done.1), channel_id=1, source_target_pairs={{0,1},{1,2},{2,3},{3,0},{4,5},{5,6},{6,7},{7,4},{8,9},{9,10},{10,1... | collective-permute-start | bytes 73736 | tf_op jit(solution)/shard_map/ppermute | solution.py:60
  119.1 3.2 %copy-start.6 = (s32[1,1,4096]{2,1,0:T(1,128)S(1)}, s32[1,1,4096]{2,1,0:T(1,128)}, u32[]{:S(2)}) copy-start(s32[1,1,4096]{2,1,0:T(1,128)} %param.22) | copy-start | bytes 49156
  119.2 27.2 %copy-start = (f32[6,6,1024]{2,1,0:T(8,128)S(1)}, f32[6,6,1024]{2,1,0:T(8,128)}, u32[]{:S(2)}) copy-start(f32[6,6,1024]{2,1,0:T(8,128)} %reshape_squeeze.6) | copy-start | bytes 442372
  119.3 27.3 %copy-start.2 = (f32[1,1,6,1024]{3,1,2,0:T(1,128)S(1)}, f32[1,1,6,1024]{3,1,2,0:T(1,128)}, u32[]{:S(2)}) copy-start(f32[1,1,6,1024]{3,1,2,0:T(1,128)} %param.18) | copy-start | bytes 73732
